TPU v7x, 32 devices: a whole 2x2x4 slice. The times are simulated.
32 devices in a mesh: parts: 2 (over x), rows: 16 (over z, y, core).
Axes of the slice: x: 2, y: 2, z: 4, core: 2. Of those that a mesh axis runs over, the one named last changes fastest.
Arguments:
- feature_bin: int32 [16384, 700], P(('parts', 'rows')), parts along dimension 0, may hold values from 0 to 255
- doc_leaf: int32 [16384], P(('parts', 'rows')), parts along dimension 0, may hold values from 0 to 31
- current_score: float32 [16384], P(('parts', 'rows')), parts along dimension 0, may hold values from -8 to 8
- relevance: int32 [16384], P(('parts', 'rows')), parts along dimension 0, may hold values from 0 to 4
- doc_rank: int32 [16384], P(('parts', 'rows')), parts along dimension 0, may hold values from 0 to 255, as said below
- query_length: int32 [64], P(('parts', 'rows')), parts along dimension 0, may hold values from 10 to 256, as said below
- feature_votes: int32 [32, 32, 20], P(('parts', 'rows')), parts along dimension 0, may hold values from 0 to 699, all different within a row
- elected: int32 [64, 40], P('parts'), parts along dimension 0, may hold values from 0 to 699, all different within a row
Outputs:
- gradient: float32 [16384], P(('parts', 'rows')), parts along dimension 0
- hessian: float32 [16384], P(('parts', 'rows')), parts along dimension 0
- vote_count: int32 [64, 700], P('parts'), parts along dimension 0
- split_gain: float32 [64, 40, 256], P('parts'), parts along dimension 0
There are 2 independent parts, one for each index of `parts`. A program takes and returns all parts, laid end to end along the dimension named above; each array names one. Nothing has to cross between parts.
Inputs may be any that keep to these rules, and one draw needn't show every extreme that they name: `query_length`: query q holds slots q * 256 to (q + 1) * 256 - 1 of the document arrays; in every draw some query has exactly 256 documents. `doc_rank`: within each query the live documents hold positions 0 to query_length - 1, each once; slots that are not live hold positions from query_length to 255. `feature_votes`: the 20 votes of one device for one leaf are different features. The 40 elected features of one leaf are different.
All inputs are finite; a program needn't handle non-finite values.
Results may differ from a plain program's by a relative error of at most 0.0003.
Values sent between devices are 32-bit elements; how exact they have to be, the bound alone decides.
No kernel may reach another device: no remote copies, remote signals or barrier semaphores. Data moves between devices by JAX's collectives and lax.ppermute only.
A program may use at most 64 MiB of HBM per device.

v0:
```python
import jax
import jax.numpy as jnp
from jax import lax
from jax.experimental import pallas as pl
from jax.experimental.pallas import tpu as pltpu
from jax.sharding import PartitionSpec as P


B = 256
LANES = 128
HALVES = B // LANES
LEVELS = 4

ridge_weight = 1.0


def cdiv(a, b):
    return -(-a // b)


def round_up(a, b):
    return cdiv(a, b) * b


def query_rows(score, level, rank, lengths, slots):
    documents = score.shape[1]
    queries = documents // slots
    gain = jnp.left_shift(1, level).astype(jnp.float32) - 1.0
    discount = 1.0 / jnp.log2(rank.astype(jnp.float32) + 2.0)
    place = lax.broadcasted_iota(jnp.int32, (1, slots), 1)
    place_discount = 1.0 / jnp.log2(place.astype(jnp.float32) + 2.0)
    gradients = []
    hessians = []
    for q in range(queries):
        lanes = slice(q * slots, (q + 1) * slots)
        live = place < lengths[q]
        live_row = live.astype(jnp.float32)
        score_row = score[:, lanes]
        gain_row = gain[:, lanes]
        discount_row = discount[:, lanes]
        level_row = jnp.where(live, level[:, lanes], -1)
        ideal_gain = jnp.zeros((1, slots), jnp.float32)
        for v in range(1, LEVELS + 1):
            count = jnp.sum((level_row >= v).astype(jnp.float32), axis=1, keepdims=True)
            ideal_gain = ideal_gain + jnp.where(
                place.astype(jnp.float32) < count, float(2 ** (v - 1)), 0.0
            )
        ideal = jnp.sum(ideal_gain * place_discount, axis=1, keepdims=True)
        scaling = 1.0 / jnp.maximum(ideal, 1.0)
        rows = jnp.concatenate(
            [score_row, gain_row, discount_row, live_row, jnp.zeros((4, slots), jnp.float32)],
            axis=0,
        )
        columns = rows.T
        step = 32
        push_sum = jnp.zeros((8, slots), jnp.float32)
        curve_sum = jnp.zeros((8, slots), jnp.float32)
        for r in range(0, slots, step):
            part = columns[r : r + step]
            gap = (part[:, 1:2] - gain_row) * part[:, 3:4]
            change = gap * jnp.abs(part[:, 2:3] - discount_row)
            lead = score_row - part[:, 0:1]
            chance = 1.0 / (1.0 + jnp.exp(jnp.where(gap > 0.0, -lead, lead)))
            push = chance * change
            curve = (1.0 - chance) * jnp.abs(push)
            for k in range(0, step, 8):
                push_sum = push_sum + push[k : k + 8]
                curve_sum = curve_sum + curve[k : k + 8]
        factor = scaling * live_row
        gradients.append(jnp.sum(push_sum, axis=0, keepdims=True) * factor)
        hessians.append(jnp.sum(curve_sum, axis=0, keepdims=True) * factor)
    return jnp.concatenate(gradients, axis=1), jnp.concatenate(hessians, axis=1)


def vmem_array(shape):
    return pltpu.VMEM(shape, jnp.float32)


def in_vmem(x):
    return pltpu.with_memory_space_constraint(x, pltpu.VMEM)


def in_hbm(x):
    return pltpu.with_memory_space_constraint(x, pltpu.HBM)


def local_stage(bins, leaf, score, level, rank, lengths, votes, elected, plan):
    features, documents = bins.shape
    leaves, picked = elected.shape
    kept = votes.shape[0]
    padded = plan["padded"]
    picks = plan["picks"]
    rows = plan["rows"]
    slots = documents // lengths.shape[0]
    group = 8 if leaves % 8 == 0 else leaves
    per_row = LANES // leaves

    piece = round_up(cdiv(features, 4), 8)
    cuts = [(f, min(piece, features - f)) for f in range(0, features, piece)]

    def body(*refs):
        sources = refs[0:8]
        grad_ref, hess_ref, packet_ref = refs[8:11]
        square, chosen_ref = refs[11:13]
        copied = refs[13:21]
        arrived = refs[21]
        bins_here, leaf_ref, score_ref, level_ref, rank_ref, length_ref, votes_ref, elected_ref = (
            copied
        )
        small = [
            pltpu.make_async_copy(sources[k], copied[k], arrived.at[len(cuts) + k - 1])
            for k in (5, 2, 3, 4, 7, 1, 6)
        ]
        fetches = [
            pltpu.make_async_copy(
                sources[0].at[pl.ds(f, size), :], bins_here.at[pl.ds(f, size), :], arrived.at[k]
            )
            for k, (f, size) in enumerate(cuts)
        ]
        for copy in small + fetches:
            copy.start()
        for copy in small:
            copy.wait()
        square[...] = jnp.zeros(square.shape, jnp.float32)
        square[0:leaves, 0:picked] = elected_ref[...].astype(jnp.float32)
        elected_t = square[...].T
        leaf_row = leaf_ref[...]
        gradient, hessian = query_rows(
            score_ref[...], level_ref[...], rank_ref[...], length_ref, slots
        )
        grad_ref[...] = gradient
        hess_ref[...] = hessian
        lane = lax.broadcasted_iota(jnp.int32, (1, documents), 1)
        starts = [0]
        for q in range(documents // slots):
            starts.append(starts[-1] + length_ref[q])

        def compact(block):
            result = block
            for q in range(1, documents // slots):
                moved = pltpu.roll(block, starts[q] - q * slots + documents, 1)
                result = jnp.where(lane >= starts[q], moved, result)
            return result

        shared = [leaf_row.astype(jnp.float32), gradient, hessian]
        shared.append(jnp.zeros((max(rows - picks, 8) - 3, documents), jnp.float32))
        shared = compact(jnp.concatenate(shared, axis=0))[0 : rows - picks]
        shared = jnp.where(lane < starts[-1], shared, 0.0)
        count = jnp.zeros((1, LANES), jnp.float32) + starts[-1].astype(jnp.float32)
        feature = lax.broadcasted_iota(jnp.int32, (padded, features), 1).astype(jnp.float32)
        for fetch in fetches:
            fetch.wait()
        table = bins_here[...].astype(jnp.float32).astype(jnp.bfloat16)
        chosen = jnp.zeros((padded, documents), jnp.float32)
        for first in range(0, leaves, group):
            hot = []
            for l in range(first, first + group):
                hot.append((elected_t[0:padded, l : l + 1] == feature).astype(jnp.float32))
            hot = jnp.concatenate(hot, axis=0).astype(jnp.bfloat16)
            found = jnp.dot(hot, table, preferred_element_type=jnp.float32)
            for i in range(group):
                chosen = jnp.where(
                    leaf_row == first + i, found[i * padded : (i + 1) * padded], chosen
                )
        chosen_ref[...] = compact(chosen)
        tail = []
        for k0 in range(0, kept, per_row):
            line = jnp.zeros((1, LANES), jnp.float32)
            for i in range(min(per_row, kept - k0)):
                values = votes_ref[k0 + i].astype(jnp.float32)
                pieces = [values]
                if i:
                    pieces.insert(0, jnp.zeros((1, i * leaves), jnp.float32))
                if (i + 1) * leaves < LANES:
                    pieces.append(jnp.zeros((1, LANES - (i + 1) * leaves), jnp.float32))
                line = line + jnp.concatenate(pieces, axis=1)
            tail.append(line)
        tail.append(count)
        spare = plan["vote_tiles"] * rows - len(tail)
        if spare:
            tail.append(jnp.zeros((spare, LANES), jnp.float32))
        tail = jnp.concatenate(tail, axis=0)
        for j in range(plan["devices"]):
            start = plan["first"][j % plan["owners"]]
            block = jnp.concatenate([chosen_ref[start : start + picks, :], shared], axis=0)
            for c in range(documents // LANES):
                packet_ref[j, c] = block[:, c * LANES : (c + 1) * LANES]
            for t in range(plan["vote_tiles"]):
                packet_ref[j, documents // LANES + t] = tail[t * rows : (t + 1) * rows]

    vmem = pl.BlockSpec(memory_space=pltpu.VMEM)
    return pl.pallas_call(
        body,
        in_specs=[pl.BlockSpec(memory_space=pltpu.HBM)] * 8,
        out_specs=[vmem] * 3,
        out_shape=[
            jax.ShapeDtypeStruct((1, documents), jnp.float32),
            jax.ShapeDtypeStruct((1, documents), jnp.float32),
            vmem_array(
                (plan["devices"], documents // LANES + plan["vote_tiles"], rows, LANES)
            ),
        ],
        scratch_shapes=[
            pltpu.VMEM((LANES, LANES), jnp.float32),
            pltpu.VMEM((padded, documents), jnp.float32),
            pltpu.VMEM((features, documents), jnp.int32),
            pltpu.VMEM((1, documents), jnp.int32),
            pltpu.VMEM((1, documents), jnp.float32),
            pltpu.VMEM((1, documents), jnp.int32),
            pltpu.VMEM((1, documents), jnp.int32),
            pltpu.SMEM(lengths.shape, jnp.int32),
            pltpu.VMEM(votes.shape, jnp.int32),
            pltpu.VMEM(elected.shape, jnp.int32),
            pltpu.SemaphoreType.DMA((len(cuts) + 7,)),
        ],
        compiler_params=pltpu.CompilerParams(vmem_limit_bytes=48 << 20),
        name="local_stage",
    )(*[in_hbm(x) for x in (bins, leaf, score, level, rank, lengths, votes, elected)])


def gain_stage(packets, where, leaves, low, high, earlier, plan):
    devices = packets.shape[0]
    picks = plan["picks"]
    units = high - low
    chunks = plan["chunks"]
    chunk = 4 if devices % 4 == 0 else 1
    even = plan["units"] % HALVES == 0

    half = cdiv(chunks, 2)
    batch = 4

    def body(where_ref, packet_ref, *refs):
        total_ref, grad_ref, hess_ref, late_ref = refs[-4:]
        out_ref = refs[len(before)]
        leaf_id = lax.broadcasted_iota(jnp.int32, (leaves, LANES), 0).astype(jnp.float32)
        bin_id = lax.broadcasted_iota(jnp.int32, (LANES, LANES), 0).astype(jnp.float32)
        local = []
        limit = []
        base = where_ref[0] % plan["owners"] * plan["units"]
        first = jnp.minimum(base // HALVES, plan["padded"] - picks)
        for i in range(low, high):
            if even:
                local.append(i // HALVES)
                limit.append(bin_id + float(i % HALVES * LANES))
            else:
                local.append(jnp.clip((base + i) // HALVES - first, 0, picks - 1))
                limit.append(bin_id + ((base + i) % HALVES * LANES).astype(jnp.float32))

        def terms(tiles):
            weights = []
            steps = [[] for _ in range(units)]
            grad_sum = jnp.zeros((leaves, LANES), jnp.float32)
            hess_sum = jnp.zeros((leaves, LANES), jnp.float32)
            for s, c, valid in tiles:
                owner = packet_ref[s, c, picks : picks + 1, :]
                if valid is not None:
                    owner = jnp.where(valid, owner, -1.0)
                mine = owner == leaf_id
                grad = jnp.where(mine, packet_ref[s, c, picks + 1 : picks + 2, :], 0.0)
                hess = jnp.where(mine, packet_ref[s, c, picks + 2 : picks + 3, :], 0.0)
                grad_sum = grad_sum + grad
                hess_sum = hess_sum + hess
                grad_high = grad.astype(jnp.bfloat16)
                hess_high = hess.astype(jnp.bfloat16)
                grad_low = (grad - grad_high.astype(jnp.float32)).astype(jnp.bfloat16)
                hess_low = (hess - hess_high.astype(jnp.float32)).astype(jnp.bfloat16)
                weights.append(
                    jnp.concatenate([grad_high, hess_high, grad_low, hess_low], axis=0)
                )
                for i in range(units):
                    value = packet_ref[s, c, pl.ds(local[i], 1), :]
                    steps[i].append((value <= limit[i]).astype(jnp.float32).astype(jnp.bfloat16))
            weight = jnp.concatenate(weights, axis=1)
            step = jnp.concatenate([jnp.concatenate(p, axis=1) for p in steps], axis=0)
            product = lax.dot_general(
                weight, step, (((1,), (1,)), ((), ())), preferred_element_type=jnp.float32
            )
            return product, grad_sum, hess_sum

        late = jnp.int32(0)
        for c in range(half, chunks):
            for s0 in range(0, devices, 16):
                flag = jnp.zeros((1, LANES), jnp.float32)
                for s in range(s0, min(s0 + 16, devices)):
                    row = plan["vote_lines"]
                    count = packet_ref[s, chunks + row // plan["rows"], row % plan["rows"], :]
                    flag = flag + jnp.where(
                        count.reshape(1, LANES) > float(c * LANES), float(1 << (s - s0)), 0.0
                    )
                flag = jnp.max(flag).astype(jnp.int32)
                for s in range(s0, min(s0 + 16, devices)):
                    late_ref[late] = s * chunks + c
                    late = late + (jnp.right_shift(flag, s - s0) & 1)

        def listed(first):
            tiles = []
            for k in range(batch):
                valid = first + k < late
                tile = jnp.where(valid, late_ref[first + k], 0)
                tiles.append((tile // chunks, tile % chunks, valid))
            return tiles

        total = grad_all = hess_all = None
        for s0 in range(0, devices + 1, chunk):
            if s0 < devices:
                tiles = [(s, c, None) for s in range(s0, s0 + chunk) for c in range(half)]
            else:
                tiles = listed(0)
            more, grad_more, hess_more = terms(tiles)
            if s0:
                more = total + more
                grad_more = grad_all + grad_more
                hess_more = hess_all + hess_more
            total, grad_all, hess_all = more, grad_more, hess_more
        total_ref[...] = total
        grad_ref[...] = grad_all
        hess_ref[...] = hess_all

        def add(k, carry):
            more, grad_more, hess_more = terms(listed(k * batch))
            total_ref[...] += more
            grad_ref[...] += grad_more
            hess_ref[...] += hess_more
            return carry

        lax.fori_loop(1, jnp.maximum((late + batch - 1) // batch, 1), add, 0)
        total = total_ref[...]
        grad_all = grad_ref[...]
        hess_all = hess_ref[...]
        prefix_grad = total[0:leaves] + total[2 * leaves : 3 * leaves]
        prefix_hess = total[leaves : 2 * leaves] + total[3 * leaves :]
        whole_grad = jnp.sum(grad_all, axis=1, keepdims=True)
        whole_hess = jnp.sum(hess_all, axis=1, keepdims=True)
        rest_grad = whole_grad - prefix_grad
        rest_hess = whole_hess - prefix_hess
        gains = (
            prefix_grad * prefix_grad / (prefix_hess + ridge_weight)
            + rest_grad * rest_grad / (rest_hess + ridge_weight)
            - whole_grad * whole_grad / (whole_hess + ridge_weight)
        )
        for i in range(units):
            out_ref[i * leaves : (i + 1) * leaves, :] = gains[:, i * LANES : (i + 1) * LANES]
        if before:
            whole_ref = refs[len(before) + 1]
            whole_ref[0 : low * leaves, :] = refs[0][...]
            whole_ref[low * leaves :, :] = out_ref[...]

    before = [] if earlier is None else [in_vmem(earlier)]
    shapes = [vmem_array((units * leaves, LANES))]
    if before:
        shapes.append(vmem_array((high * leaves, LANES)))
    vmem = pl.BlockSpec(memory_space=pltpu.VMEM)
    return pl.pallas_call(
        body,
        in_specs=[pl.BlockSpec(memory_space=pltpu.SMEM), vmem] + [vmem] * len(before),
        out_specs=[vmem] * len(shapes),
        out_shape=shapes,
        scratch_shapes=[
            pltpu.VMEM((4 * leaves, units * LANES), jnp.float32),
            pltpu.VMEM((leaves, LANES), jnp.float32),
            pltpu.VMEM((leaves, LANES), jnp.float32),
            pltpu.SMEM((devices * chunks + batch,), jnp.int32),
        ],
        compiler_params=pltpu.CompilerParams(vmem_limit_bytes=48 << 20),
        name="gain_stage",
    )(where, in_vmem(packets), *before)


def vote_stage(packets, before, sources, last, features, leaves, kept, plan):
    rows = plan["rows"]
    lines = plan["vote_lines"]
    step = 128
    depth = round_up(features, step)
    inputs = [in_vmem(packets)] + ([] if before is None else [in_vmem(before)])

    def body(packet_ref, *refs):
        out_ref, count = refs[-2:] if last else (None, refs[-1])
        lane = lax.broadcasted_iota(jnp.int32, (1, LANES), 1)

        feature = lax.broadcasted_iota(jnp.int32, (step, LANES), 0).astype(jnp.float32)
        feature = feature.astype(jnp.bfloat16)
        one = jnp.ones((step, LANES), jnp.bfloat16)
        zero = jnp.zeros((step, LANES), jnp.bfloat16)

        def block(index, carry):
            start = pl.multiple_of(index * step, step)
            offset = jnp.float32(index * step)
            total = jnp.zeros((step, LANES), jnp.float32)
            if before is not None:
                total = refs[0][pl.ds(start, step), :]
            for s0 in range(0, len(sources), 16):
                found = jnp.zeros((step, LANES), jnp.bfloat16)
                for s in sources[s0 : s0 + 16]:
                    for line in range(lines):
                        row = line % rows
                        values = packet_ref[s, plan["chunks"] + line // rows, row : row + 1, :]
                        inside = kept * leaves - line * LANES
                        if inside < LANES:
                            values = jnp.where(lane < inside, values, -1.0)
                        values = jnp.clip(values - offset, -1.0, float(step))
                        values = jnp.broadcast_to(values, (16, LANES)).astype(jnp.bfloat16)
                        values = jnp.concatenate([values] * (step // 16), axis=0)
                        found = found + jnp.where(values == feature, one, zero)
                total = total + found.astype(jnp.float32)
            count[pl.ds(start, step), :] = total
            return carry

        lax.fori_loop(0, depth // step, block, 0)
        if last:
            turned = count[...].T
            summed = turned[0:leaves]
            for i in range(1, LANES // leaves):
                summed = summed + turned[i * leaves : (i + 1) * leaves]
            out_ref[...] = summed[:, 0:features].astype(jnp.int32)

    vmem = pl.BlockSpec(memory_space=pltpu.VMEM)
    if last:
        out_shape = jax.ShapeDtypeStruct((leaves, features), jnp.int32)
        scratch = [pltpu.VMEM((depth, LANES), jnp.float32)]
    else:
        out_shape = vmem_array((depth, LANES))
        scratch = []
    return pl.pallas_call(
        body,
        in_specs=[vmem] * len(inputs),
        out_specs=vmem,
        out_shape=out_shape,
        scratch_shapes=scratch,
        compiler_params=pltpu.CompilerParams(vmem_limit_bytes=48 << 20),
        cost_estimate=pl.CostEstimate(flops=20_000_000, bytes_accessed=400_000, transcendentals=0),
        name="vote_stage",
    )(*inputs)


def pack_stage(arrays):
    def body(*refs):
        start = 0
        for ref in refs[:-1]:
            refs[-1][start : start + ref.shape[0], :] = ref[...]
            start += ref.shape[0]

    vmem = pl.BlockSpec(memory_space=pltpu.VMEM)
    return pl.pallas_call(
        body,
        in_specs=[vmem] * len(arrays),
        out_specs=vmem,
        out_shape=vmem_array((sum(a.shape[0] for a in arrays), arrays[0].shape[1])),
        compiler_params=pltpu.CompilerParams(vmem_limit_bytes=48 << 20),
        name="pack_stage",
    )(*[in_vmem(a) for a in arrays])


def place_stage(blocks, pieces, where, leaves, picked, plan):
    units = plan["units"]
    owners = plan["owners"]
    step = 8 if leaves % 8 == 0 else leaves

    rows = step * picked
    groups = leaves // step

    def body(where_ref, *refs):
        out_ref, planes, done = refs[-3:]
        here = where_ref[0] % owners
        odd = here & 1
        owner = []
        for _, _, even_tag, odd_tag, _, _, other in pieces:
            if not plan["doubling"]:
                owner.append(even_tag)
            elif not other:
                owner.append(here ^ jnp.where(odd == 1, odd_tag, even_tag))
            else:
                owner.append(here ^ 1 ^ jnp.where(odd == 1, even_tag, odd_tag))
        copies = []
        for g in range(groups):
            for index, (number, base, _, _, low, high, _) in enumerate(pieces):
                for i in range(low, high):

                    def write(index=index, ref=refs[number], i=i, low=low, base=base):
                        if units % HALVES == 0:
                            half = i % HALVES
                            pick = owner[index] * (units // HALVES) + i // HALVES
                        else:
                            half = (owner[index] * units + i) % HALVES
                            pick = (owner[index] * units + i) // HALVES
                        start = base + (i - low) * leaves + g * step
                        planes[half, pl.ds(g * rows + pick, step, stride=picked), :] = ref[
                            start : start + step, :
                        ]

                    if owners * units == picked * HALVES:
                        write()
                    else:
                        pl.when(owner[index] * units + i < picked * HALVES)(write)
            for half in range(HALVES):
                copy = pltpu.make_async_copy(
                    planes.at[half, pl.ds(g * rows, rows), :],
                    out_ref.at[pl.ds(g * rows, rows), pl.ds(half * LANES, LANES)],
                    done.at[g * HALVES + half],
                )
                copy.start()
                copies.append(copy)
        for copy in copies:
            copy.wait()

    vmem = pl.BlockSpec(memory_space=pltpu.VMEM)
    return pl.pallas_call(
        body,
        in_specs=[pl.BlockSpec(memory_space=pltpu.SMEM)] + [vmem] * len(blocks),
        out_specs=pl.BlockSpec(memory_space=pltpu.HBM),
        out_shape=jax.ShapeDtypeStruct((leaves * picked, B), jnp.float32),
        scratch_shapes=[
            pltpu.VMEM((HALVES, leaves * picked, LANES), jnp.float32),
            pltpu.SemaphoreType.DMA((groups * HALVES,)),
        ],
        compiler_params=pltpu.CompilerParams(vmem_limit_bytes=48 << 20),
        name="place_stage",
    )(where, *[in_vmem(b) for b in blocks]).reshape(leaves, picked, B)


def solution(mesh):
    devices = mesh.shape["rows"]

    def on_device(
        feature_bin, doc_leaf, current_score, relevance, doc_rank, query_length, feature_votes,
        elected,
    ):
        documents, features = feature_bin.shape
        leaves, picked = elected.shape
        kept = feature_votes.shape[2]
        doubling = devices >= 8 and devices & (devices - 1) == 0
        owners = devices // 2 if doubling else devices
        units = max(cdiv(picked * HALVES, owners), 2)
        padded = round_up(picked, 8)
        picks = max(
            (j * units + units - 1) // HALVES - (j * units) // HALVES + 1 for j in range(owners)
        )
        rows = round_up(picks + 3, 8)
        plan = {
            "devices": devices,
            "doubling": doubling,
            "owners": owners,
            "units": units,
            "picks": picks,
            "padded": padded,
            "first": [min(j * units // HALVES, padded - picks) for j in range(owners)],
            "rows": rows,
            "chunks": documents // LANES,
            "vote_lines": cdiv(kept * leaves, LANES),
            "vote_tiles": cdiv(cdiv(kept * leaves, LANES) + 1, rows),
        }
        where = lax.axis_index("rows").astype(jnp.int32).reshape(1)
        gradient, hessian, packets = local_stage(
            feature_bin.T,
            doc_leaf.reshape(1, -1),
            current_score.reshape(1, -1),
            relevance.reshape(1, -1),
            doc_rank.reshape(1, -1),
            query_length,
            feature_votes.transpose(2, 0, 1),
            elected,
            plan,
        )
        received = lax.all_to_all(packets, "rows", 0, 0)
        counters = (features, leaves, kept, plan)
        third = cdiv(devices, 3)
        shares = [range(min(k * third, devices), min((k + 1) * third, devices)) for k in range(3)]
        cut = units * 4 // 5
        if units % HALVES == 0:
            cut = max(cut // HALVES, 1) * HALVES if units > HALVES else 1
        (part,) = gain_stage(received, where, leaves, 0, cut, None, plan)
        rest, block = gain_stage(received, where, leaves, cut, units, part, plan)
        votes = vote_stage(received, None, shares[0], False, *counters)
        if doubling:
            far = [1 << b for b in reversed(range(1, owners.bit_length() - 1))]
            twin = list(far)
            twin[-2:] = twin[-2:][::-1]
            pairs = [
                [(i, i ^ (twin[p] if i & 1 else far[p])) for i in range(devices)]
                for p in range(len(far))
            ]
            sibling = [(i, i ^ 1) for i in range(devices)]

            def send(items, p):
                return [
                    (
                        lax.ppermute(b, "rows", pairs[p]),
                        [(even ^ far[p], odd ^ twin[p], low, high) for even, odd, low, high in spans],
                    )
                    for b, spans in items
                ]

            def cross(items):
                return [(lax.ppermute(b, "rows", sibling), spans) for b, spans in items]

            def after(items, other):
                arrays, other = lax.optimization_barrier(([item[0] for item in items], other))
                return [(b, item[1]) for b, item in zip(arrays, items)], other

            def packed_after(items, votes):
                packed = pack_stage([b for b, _ in items])
                packed = (packed, sum([spans for _, spans in items], []))
                return after([packed], votes)

            own = [(block, [(0, 0, 0, units)])]
            first = send([(part, [(0, 0, 0, cut)])], 0)
            second = send([(rest, [(0, 0, cut, units)])], 0)
            first, votes = after(first, votes)
            votes = vote_stage(received, votes, shares[1], False, *counters)
            items = own + first + second
            for p in range(1, len(far)):
                if p < len(far) - 1:
                    items = items + send(items, p)
                    continue
                moved = send(own, p)
                moved = moved + send(items[1:-1], p)
                moved = moved + send(items[-1:], p)
                votes = vote_stage(received, votes, shares[2], True, *counters)
                packed, votes = packed_after(items, votes)
                crossed = cross(packed)
                crossed = crossed + cross(moved[:1])
                crossed = crossed + cross(moved[1:-1])
                crossed = crossed + cross(moved[-1:])
                items = items + moved
            if len(far) == 1:
                votes = vote_stage(received, votes, shares[2], True, *counters)
                crossed = cross(items)
            pieces = []
            blocks = []
            for side, group in ((False, items), (True, crossed)):
                for b, spans in group:
                    base = 0
                    for even, odd, low, high in spans:
                        pieces.append((len(blocks), base, even, odd, low, high, side))
                        base += (high - low) * leaves
                    blocks.append(b)
        else:
            votes = vote_stage(received, votes, range(third, devices), True, *counters)
            gathered = lax.all_gather(block, "rows", axis=0)
            blocks = [gathered[j] for j in range(devices)]
            pieces = [(j, 0, j, j, 0, units, False) for j in range(devices)]
        split_gain = place_stage(blocks, pieces, where, leaves, picked, plan)
        return gradient.reshape(-1), hessian.reshape(-1), votes, split_gain


    return jax.shard_map(
        on_device,
        mesh=mesh,
        in_specs=(
            P(("parts", "rows"), None),
            P(("parts", "rows")),
            P(("parts", "rows")),
            P(("parts", "rows")),
            P(("parts", "rows")),
            P(("parts", "rows")),
            P(("parts", "rows"), None, None),
            P("parts", None),
        ),
        out_specs=(
            P(("parts", "rows")),
            P(("parts", "rows")),
            P("parts", None),
            P("parts", None, None),
        ),
        check_vma=False,
    )
```

profile of v0, /device:TPU:0, one launch (start us, length us, event | category | flops | bytes accessed | tf_op | source)
XLA Modules:
  0.0 45.0 jit_solution(12860546043852667768)
XLA Ops:
  0.6 3.9 %local_stage.1 = (f32[1,512]{1,0:T(1,128)}, f32[1,512]{1,0:T(1,128)}, f32[16,5,8,128]{3,2,1,0:T(8,128)}) custom-call(s32[700,512]{1,0:T(8,128)} %bitcast.10, s32[1,512]{1,0:T(1,128)} %bitcast.13, f32[1,512]{1,0:T(1,128)} %bitcast.14, s32[1,512]{1,0:T(1,128)} %bitcast.15, s32[1,512]{1,0:T(1,128)} %bitcast.16, s32[2]{0:T(128)} %refs_5_.1, ...), custom_call_target="tpu_custom_call" | custom-call | tf_op jit(solution)/shard_map/local_stage/pallas_call | solution.py:192
  4.5 7.4 %all-to-all-start = ((f32[16,5,8,128]{3,2,1,0:T(8,128)}), f32[16,5,8,128]{3,2,1,0:T(8,128)S(1)}, u32[]{:S(2)}, u32[]{:S(2)}) async-start(f32[16,5,8,128]{3,2,1,0:T(8,128)} %get-tuple-element.15), calls=%async_computation | async-start | bytes 655360 | tf_op jit(solution)/shard_map/all_to_all | solution.py:563
  11.9 11.1 %all-to-all-done.packet_ref = f32[16,5,8,128]{3,2,1,0:T(8,128)S(1)} async-done(((f32[16,5,8,128]{3,2,1,0:T(8,128)}), f32[16,5,8,128]{3,2,1,0:T(8,128)S(1)}, u32[]{:S(2)}, u32[]{:S(2)}) %all-to-all-start) | async-done | bytes 327712 | tf_op jit(solution)/shard_map/all_to_all | solution.py:563
  23.0 3.3 %gain_stage.2.refs_0_ = f32[256,128]{1,0:T(8,128)S(1)} custom-call(s32[1]{0:T(128)} %bitcast.8.where_ref, f32[16,5,8,128]{3,2,1,0:T(8,128)S(1)} %all-to-all-done.packet_ref), custom_call_target="tpu_custom_call" | custom-call | tf_op jit(solution)/shard_map/gain_stage/pallas_call | solution.py:353
  26.3 0.2 collective-permute-start
  26.6 1.0 %gain_stage.3 = (f32[64,128]{1,0:T(8,128)S(1)}, f32[320,128]{1,0:T(8,128)S(1)}) custom-call(s32[1]{0:T(128)} %bitcast.8.where_ref, f32[16,5,8,128]{3,2,1,0:T(8,128)S(1)} %all-to-all-done.packet_ref, f32[256,128]{1,0:T(8,128)S(1)} %gain_stage.2.refs_0_), custom_call_target="tpu_custom_call" | custom-call | tf_op jit(solution)/shard_map/gain_stage/pallas_call | solution.py:353
  27.6 1.9 %collective-permute-start.1 = (f32[64,128]{1,0:T(8,128)S(1)}, f32[64,128]{1,0:T(8,128)S(1)}, u32[]{:S(2)}, u32[]{:S(2)}) collective-permute-start(f32[64,128]{1,0:T(8,128)S(1)} %get-tuple-element.18), channel_id=1, source_target_pairs={{0,4},{1,3},{2,6},{3,1},{4,0},{5,7},{6,2},{7,5},{8,12},{9,11},{10,... | collective-permute-start | bytes 98312 | tf_op jit(solution)/shard_map/ppermute | solution.py:586
  29.5 0.0 collective-permute-start.2
  29.6 0.8 %vote_stage.3.refs_0_ = f32[768,128]{1,0:T(8,128)S(1)} custom-call(f32[16,5,8,128]{3,2,1,0:T(8,128)S(1)} %all-to-all-done.packet_ref), custom_call_target="tpu_custom_call" | custom-call | flops 20000000 | bytes 400000 | tf_op jit(solution)/shard_map/vote_stage/pallas_call | solution.py:423
  30.3 1.0 %collective-permute-done.refs_1_ = f32[256,128]{1,0:T(8,128)S(1)} collective-permute-done((f32[256,128]{1,0:T(8,128)S(1)}, f32[256,128]{1,0:T(8,128)S(1)}, u32[]{:S(2)}, u32[]{:S(2)}) %collective-permute-start) | collective-permute-done | bytes 131104 | tf_op jit(solution)/shard_map/ppermute | solution.py:586
  31.4 0.8 %vote_stage.4.refs_0_ = f32[768,128]{1,0:T(8,128)S(1)} custom-call(f32[16,5,8,128]{3,2,1,0:T(8,128)S(1)} %all-to-all-done.packet_ref, f32[768,128]{1,0:T(8,128)S(1)} %vote_stage.3.refs_0_), custom_call_target="tpu_custom_call" | custom-call | flops 20000000 | bytes 400000 | tf_op jit(solution)/shard_map/vote_stage/pallas_call | solution.py:423
  32.2 1.4 %vote_stage.5 = s32[32,700]{1,0:T(8,128)} custom-call(f32[16,5,8,128]{3,2,1,0:T(8,128)S(1)} %all-to-all-done.packet_ref, f32[768,128]{1,0:T(8,128)S(1)} %vote_stage.4.refs_0_), custom_call_target="tpu_custom_call" | custom-call | flops 20000000 | bytes 400000 | tf_op jit(solution)/shard_map/vote_stage/pallas_call | solution.py:423
  33.5 0.0 collective-permute-done.1.refs_2_
  33.6 0.1 collective-permute-start.5
  33.6 1.1 %collective-permute-start.3 = (f32[256,128]{1,0:T(8,128)S(1)}, f32[256,128]{1,0:T(8,128)S(1)}, u32[]{:S(2)}, u32[]{:S(2)}) collective-permute-start(f32[256,128]{1,0:T(8,128)S(1)} %collective-permute-done.refs_1_), channel_id=1, source_target_pairs={{0,2},{1,5},{2,0},{3,7},{4,6},{5,1},{6,4},{7,3},{8,10},{9,13},{10,... | collective-permute-start | bytes 393224 | tf_op jit(solution)/shard_map/ppermute | solution.py:586
  34.7 0.2 collective-permute-done.2.refs_3_
  34.9 0.0 collective-permute-start.6
  34.9 3.8 %collective-permute-done.3.refs_4_ = f32[256,128]{1,0:T(8,128)S(1)} collective-permute-done((f32[256,128]{1,0:T(8,128)S(1)}, f32[256,128]{1,0:T(8,128)S(1)}, u32[]{:S(2)}, u32[]{:S(2)}) %collective-permute-start.3) | collective-permute-done | bytes 131104 | tf_op jit(solution)/shard_map/ppermute | solution.py:586
  38.7 0.0 collective-permute-start.7
  38.7 1.0 %collective-permute-start.4 = (f32[64,128]{1,0:T(8,128)S(1)}, f32[64,128]{1,0:T(8,128)S(1)}, u32[]{:S(2)}, u32[]{:S(2)}) collective-permute-start(f32[64,128]{1,0:T(8,128)S(1)} %collective-permute-done.1.refs_2_), channel_id=1, source_target_pairs={{0,2},{1,5},{2,0},{3,7},{4,6},{5,1},{6,4},{7,3},{8,10},{9,13},{10,... | collective-permute-start | bytes 98312 | tf_op jit(solution)/shard_map/ppermute | solution.py:586
  39.7 2.9 %collective-permute-done.4.refs_5_ = f32[64,128]{1,0:T(8,128)S(1)} collective-permute-done((f32[64,128]{1,0:T(8,128)S(1)}, f32[64,128]{1,0:T(8,128)S(1)}, u32[]{:S(2)}, u32[]{:S(2)}) %collective-permute-start.4) | collective-permute-done | bytes 32800 | tf_op jit(solution)/shard_map/ppermute | solution.py:586
  42.6 0.0 collective-permute-start.8
  42.6 1.2 %collective-permute-done.8.refs_9_ = f32[64,128]{1,0:T(8,128)S(1)} collective-permute-done((f32[64,128]{1,0:T(8,128)S(1)}, f32[64,128]{1,0:T(8,128)S(1)}, u32[]{:S(2)}, u32[]{:S(2)}) %collective-permute-start.8) | collective-permute-done | bytes 32800 | tf_op jit(solution)/shard_map/ppermute | solution.py:593
  43.8 0.0 collective-permute-done.6.refs_7_
  43.8 0.0 collective-permute-done.7.refs_8_
  43.8 0.0 collective-permute-done.5.refs_6_
  43.8 1.2 %place_stage.1 = f32[1280,256]{1,0:T(8,128)} custom-call(s32[1]{0:T(128)} %bitcast.8.where_ref, f32[320,128]{1,0:T(8,128)S(1)} %get-tuple-element.16.refs_0_, f32[256,128]{1,0:T(8,128)S(1)} %collective-permute-done.refs_1_, f32[64,128]{1,0:T(8,128)S(1)} %collective-permute-done.1.refs_2_, f32[320,128]{1,0:T(8,128)S(1)} %collective-permute-done.2.refs_3_, ...), custom_call_target="tpu_custom_call" | custom-call | tf_op jit(solution)/shard_map/place_stage/pallas_call | solution.py:506
  (1 shorter events, 0.0 us)
Async XLA Ops:
  4.5 18.5 %all-to-all-start = ((f32[16,5,8,128]{3,2,1,0:T(8,128)}), f32[16,5,8,128]{3,2,1,0:T(8,128)S(1)}, u32[]{:S(2)}, u32[]{:S(2)}) async-start(f32[16,5,8,128]{3,2,1,0:T(8,128)} %get-tuple-element.15), calls=%async_computation | async-start | bytes 655360 | tf_op jit(solution)/shard_map/all_to_all | solution.py:563
  26.3 5.0 %collective-permute-start = (f32[256,128]{1,0:T(8,128)S(1)}, f32[256,128]{1,0:T(8,128)S(1)}, u32[]{:S(2)}, u32[]{:S(2)}) collective-permute-start(f32[256,128]{1,0:T(8,128)S(1)} %gain_stage.2.refs_0_), channel_id=1, source_target_pairs={{0,4},{1,3},{2,6},{3,1},{4,0},{5,7},{6,2},{7,5},{8,12},{9,11},{10,... | collective-permute-start | bytes 393224 | tf_op jit(solution)/shard_map/ppermute | solution.py:586
  27.6 5.9 %collective-permute-start.1 = (f32[64,128]{1,0:T(8,128)S(1)}, f32[64,128]{1,0:T(8,128)S(1)}, u32[]{:S(2)}, u32[]{:S(2)}) collective-permute-start(f32[64,128]{1,0:T(8,128)S(1)} %get-tuple-element.18), channel_id=1, source_target_pairs={{0,4},{1,3},{2,6},{3,1},{4,0},{5,7},{6,2},{7,5},{8,12},{9,11},{10,... | collective-permute-start | bytes 98312 | tf_op jit(solution)/shard_map/ppermute | solution.py:586
  29.5 5.3 %collective-permute-start.2 = (f32[320,128]{1,0:T(8,128)S(1)}, f32[320,128]{1,0:T(8,128)S(1)}, u32[]{:S(2)}, u32[]{:S(2)}) collective-permute-start(f32[320,128]{1,0:T(8,128)S(1)} %get-tuple-element.16.refs_0_), channel_id=1, source_target_pairs={{0,2},{1,5},{2,0},{3,7},{4,6},{5,1},{6,4},{7,3},{8,10},{9,13},{10,... | collective-permute-start | bytes 491528 | tf_op jit(solution)/shard_map/ppermute | solution.py:586
  33.6 10.2 %collective-permute-start.5 = (f32[640,128]{1,0:T(8,128)S(1)}, f32[640,128]{1,0:T(8,128)S(1)}, u32[]{:S(2)}, u32[]{:S(2)}) collective-permute-start(f32[640,128]{1,0:T(8,128)S(1)} %pack_stage.1), channel_id=1, source_target_pairs={{0,1},{1,0},{2,3},{3,2},{4,5},{5,4},{6,7},{7,6},{8,9},{9,8},{10,11... | collective-permute-start | bytes 983048 | tf_op jit(solution)/shard_map/ppermute | solution.py:593
  33.6 5.0 %collective-permute-start.3 = (f32[256,128]{1,0:T(8,128)S(1)}, f32[256,128]{1,0:T(8,128)S(1)}, u32[]{:S(2)}, u32[]{:S(2)}) collective-permute-start(f32[256,128]{1,0:T(8,128)S(1)} %collective-permute-done.refs_1_), channel_id=1, source_target_pairs={{0,2},{1,5},{2,0},{3,7},{4,6},{5,1},{6,4},{7,3},{8,10},{9,13},{10,... | collective-permute-start | bytes 393224 | tf_op jit(solution)/shard_map/ppermute | solution.py:586
  34.9 8.9 %collective-permute-start.6 = (f32[320,128]{1,0:T(8,128)S(1)}, f32[320,128]{1,0:T(8,128)S(1)}, u32[]{:S(2)}, u32[]{:S(2)}) collective-permute-start(f32[320,128]{1,0:T(8,128)S(1)} %collective-permute-done.2.refs_3_), channel_id=1, source_target_pairs={{0,1},{1,0},{2,3},{3,2},{4,5},{5,4},{6,7},{7,6},{8,9},{9,8},{10,11... | collective-permute-start | bytes 491528 | tf_op jit(solution)/shard_map/ppermute | solution.py:593
  38.7 5.1 %collective-permute-start.7 = (f32[256,128]{1,0:T(8,128)S(1)}, f32[256,128]{1,0:T(8,128)S(1)}, u32[]{:S(2)}, u32[]{:S(2)}) collective-permute-start(f32[256,128]{1,0:T(8,128)S(1)} %collective-permute-done.3.refs_4_), channel_id=1, source_target_pairs={{0,1},{1,0},{2,3},{3,2},{4,5},{5,4},{6,7},{7,6},{8,9},{9,8},{10,11... | collective-permute-start | bytes 393224 | tf_op jit(solution)/shard_map/ppermute | solution.py:593
  38.7 3.9 %collective-permute-start.4 = (f32[64,128]{1,0:T(8,128)S(1)}, f32[64,128]{1,0:T(8,128)S(1)}, u32[]{:S(2)}, u32[]{:S(2)}) collective-permute-start(f32[64,128]{1,0:T(8,128)S(1)} %collective-permute-done.1.refs_2_), channel_id=1, source_target_pairs={{0,2},{1,5},{2,0},{3,7},{4,6},{5,1},{6,4},{7,3},{8,10},{9,13},{10,... | collective-permute-start | bytes 98312 | tf_op jit(solution)/shard_map/ppermute | solution.py:586
  42.6 1.2 %collective-permute-start.8 = (f32[64,128]{1,0:T(8,128)S(1)}, f32[64,128]{1,0:T(8,128)S(1)}, u32[]{:S(2)}, u32[]{:S(2)}) collective-permute-start(f32[64,128]{1,0:T(8,128)S(1)} %collective-permute-done.4.refs_5_), channel_id=1, source_target_pairs={{0,1},{1,0},{2,3},{3,2},{4,5},{5,4},{6,7},{7,6},{8,9},{9,8},{10,11... | collective-permute-start | bytes 98312 | tf_op jit(solution)/shard_map/ppermute | solution.py:593
where the time goes:
time: 45.2 us; the launch traced here: 45 us
  waiting for transfers between devices  20.2 us (45%)
  Pallas kernels  12.4 us (27%)
  starting transfers between devices  11.7 us (26%)
  between operations  0.69 us (2%)
    all_to_all x1, waiting for transfers between devices, on_device(): received = lax.all_to_all(packets, 'rows', 0, 0)  11.1 us
    ppermute x5, waiting for transfers between devices, send(): lax.ppermute(b, 'rows', pairs[p])  7.95 us
    all_to_all x1, starting transfers between devices, on_device(): received = lax.all_to_all(packets, 'rows', 0, 0)  7.43 us
    pallas_call x2, Pallas kernels, gain_stage(): pl.pallas_call(body, in_specs=[pl.BlockSpec(memory_space=pltpu.SMEM), vme...  4.37 us
    ppermute x5, starting transfers between devices, send(): lax.ppermute(b, 'rows', pairs[p])  4.2 us
    pallas_call x1, Pallas kernels, local_stage(): pl.pallas_call(body, in_specs=[pl.BlockSpec(memory_space=pltpu.HBM)] * 8,...  3.86 us
    pallas_call x3, Pallas kernels, vote_stage(): pl.pallas_call(body, in_specs=[vmem] * len(inputs), out_specs=vmem, out_s...  2.93 us
    ppermute x4, waiting for transfers between devices, cross(): return [(lax.ppermute(b, 'rows', sibling), spans) for b, spans in items]  1.21 us
  transfers between devices with their start and end apart: 10, of which 6 were waited for; matrix products, arithmetic and copies ran while one was open for 0% of the time, Pallas kernels for 9%

commit v1 on v0

--- a/solution.py
+++ b/solution.py
@@ -225,6 +225,7 @@
     chunks = plan["chunks"]
     chunk = 4 if devices % 4 == 0 else 1
     even = plan["units"] % HALVES == 0
+    plain = units // 2 // HALVES * HALVES if even else 0
 
     half = cdiv(chunks, 2)
     batch = 4
@@ -234,6 +235,7 @@
         out_ref = refs[len(before)]
         leaf_id = lax.broadcasted_iota(jnp.int32, (leaves, LANES), 0).astype(jnp.float32)
         bin_id = lax.broadcasted_iota(jnp.int32, (LANES, LANES), 0).astype(jnp.float32)
+        across = lax.broadcasted_iota(jnp.int32, (LANES, LANES), 1).astype(jnp.float32)
         local = []
         limit = []
         base = where_ref[0] % plan["owners"] * plan["units"]
@@ -241,17 +243,32 @@
         for i in range(low, high):
             if even:
                 local.append(i // HALVES)
-                limit.append(bin_id + float(i % HALVES * LANES))
+                limit.append((across if i - low < plain else bin_id) + float(i % HALVES * LANES))
             else:
                 local.append(jnp.clip((base + i) // HALVES - first, 0, picks - 1))
                 limit.append(bin_id + ((base + i) % HALVES * LANES).astype(jnp.float32))
 
+        def turned(tiles):
+            rows = plan["rows"]
+            result = []
+            for t0 in range(0, len(tiles), LANES // rows):
+                some = [packet_ref[s, c] for s, c, _ in tiles[t0 : t0 + LANES // rows]]
+                spare = LANES - len(some) * rows
+                if spare:
+                    some.append(jnp.zeros((spare, LANES), jnp.float32))
+                square = jnp.concatenate(some, axis=0).T
+                for t in range(min(len(tiles) - t0, LANES // rows)):
+                    result.append(square[:, t * rows : (t + 1) * rows])
+            return result
+
         def terms(tiles):
             weights = []
-            steps = [[] for _ in range(units)]
+            steps = []
+            others = [[] for _ in range(units - plain)]
+            columns = turned(tiles) if plain else [None] * len(tiles)
             grad_sum = jnp.zeros((leaves, LANES), jnp.float32)
             hess_sum = jnp.zeros((leaves, LANES), jnp.float32)
-            for s, c, valid in tiles:
+            for (s, c, valid), column in zip(tiles, columns):
                 owner = packet_ref[s, c, picks : picks + 1, :]
                 if valid is not None:
                     owner = jnp.where(valid, owner, -1.0)
@@ -267,14 +284,34 @@
                 weights.append(
                     jnp.concatenate([grad_high, hess_high, grad_low, hess_low], axis=0)
                 )
-                for i in range(units):
+                step = []
+                for i in range(plain):
+                    k = local[i]
+                    value = jnp.broadcast_to(column[:, k : k + 1], (LANES, LANES))
+                    step.append((value <= limit[i]).astype(jnp.float32).astype(jnp.bfloat16))
+                if plain:
+                    steps.append(jnp.concatenate(step, axis=1))
+                for i in range(plain, units):
                     value = packet_ref[s, c, pl.ds(local[i], 1), :]
-                    steps[i].append((value <= limit[i]).astype(jnp.float32).astype(jnp.bfloat16))
+                    others[i - plain].append(
+                        (value <= limit[i]).astype(jnp.float32).astype(jnp.bfloat16)
+                    )
             weight = jnp.concatenate(weights, axis=1)
-            step = jnp.concatenate([jnp.concatenate(p, axis=1) for p in steps], axis=0)
-            product = lax.dot_general(
-                weight, step, (((1,), (1,)), ((), ())), preferred_element_type=jnp.float32
-            )
+            product = []
+            if plain:
+                step = jnp.concatenate(steps, axis=0)
+                product.append(jnp.dot(weight, step, preferred_element_type=jnp.float32))
+            if plain < units:
+                step = jnp.concatenate([jnp.concatenate(p, axis=1) for p in others], axis=0)
+                product.append(
+                    lax.dot_general(
+                        weight,
+                        step,
+                        (((1,), (1,)), ((), ())),
+                        preferred_element_type=jnp.float32,
+                    )
+                )
+            product = jnp.concatenate(product, axis=1)
             return product, grad_sum, hess_sum
 
         late = jnp.int32(0)

time: 45.2 us -> 44.7 us (0.989)
  Pallas kernels: 12.4 us -> 11.8 us
    pallas_call x2, Pallas kernels: 4.37 us -> 3.82 us  [gain_stage(): pl.pallas_call(body, in_specs=[pl.BlockSpec(memory_space=pltpu.SMEM), vme...]
where the time goes in v1:
time: 44.7 us; the launch traced here: 44.4 us
  waiting for transfers between devices  20.2 us (45%)
  Pallas kernels  11.8 us (26%)
  starting transfers between devices  11.7 us (26%)
  between operations  0.69 us (2%)
    all_to_all x1, waiting for transfers between devices, on_device(): received = lax.all_to_all(packets, 'rows', 0, 0)  11.1 us
    ppermute x5, waiting for transfers between devices, send(): lax.ppermute(b, 'rows', pairs[p])  7.95 us
    all_to_all x1, starting transfers between devices, on_device(): received = lax.all_to_all(packets, 'rows', 0, 0)  7.43 us
    ppermute x5, starting transfers between devices, send(): lax.ppermute(b, 'rows', pairs[p])  4.2 us
    pallas_call x1, Pallas kernels, local_stage(): pl.pallas_call(body, in_specs=[pl.BlockSpec(memory_space=pltpu.HBM)] * 8,...  3.86 us
    pallas_call x2, Pallas kernels, gain_stage(): pl.pallas_call(body, in_specs=[pl.BlockSpec(memory_space=pltpu.SMEM), vme...  3.82 us
    pallas_call x3, Pallas kernels, vote_stage(): pl.pallas_call(body, in_specs=[vmem] * len(inputs), out_specs=vmem, out_s...  2.93 us
    ppermute x4, waiting for transfers between devices, cross(): return [(lax.ppermute(b, 'rows', sibling), spans) for b, spans in items]  1.21 us
  transfers between devices with their start and end apart: 10, of which 6 were waited for; matrix products, arithmetic and copies ran while one was open for 0% of the time, Pallas kernels for 9%

profile of v1, /device:TPU:0, one launch (start us, length us, event | category | flops | bytes accessed | tf_op | source)
XLA Modules:
  0.0 44.4 jit_solution(340096214987479951)
XLA Ops:
  0.6 3.9 %local_stage.1 = (f32[1,512]{1,0:T(1,128)}, f32[1,512]{1,0:T(1,128)}, f32[16,5,8,128]{3,2,1,0:T(8,128)}) custom-call(s32[700,512]{1,0:T(8,128)} %bitcast.10, s32[1,512]{1,0:T(1,128)} %bitcast.13, f32[1,512]{1,0:T(1,128)} %bitcast.14, s32[1,512]{1,0:T(1,128)} %bitcast.15, s32[1,512]{1,0:T(1,128)} %bitcast.16, s32[2]{0:T(128)} %refs_5_.1, ...), custom_call_target="tpu_custom_call" | custom-call | tf_op jit(solution)/shard_map/local_stage/pallas_call | solution.py:192
  4.5 7.4 %all-to-all-start = ((f32[16,5,8,128]{3,2,1,0:T(8,128)}), f32[16,5,8,128]{3,2,1,0:T(8,128)S(1)}, u32[]{:S(2)}, u32[]{:S(2)}) async-start(f32[16,5,8,128]{3,2,1,0:T(8,128)} %get-tuple-element.15), calls=%async_computation | async-start | bytes 655360 | tf_op jit(solution)/shard_map/all_to_all | solution.py:600
  11.9 11.1 %all-to-all-done.packet_ref = f32[16,5,8,128]{3,2,1,0:T(8,128)S(1)} async-done(((f32[16,5,8,128]{3,2,1,0:T(8,128)}), f32[16,5,8,128]{3,2,1,0:T(8,128)S(1)}, u32[]{:S(2)}, u32[]{:S(2)}) %all-to-all-start) | async-done | bytes 327712 | tf_op jit(solution)/shard_map/all_to_all | solution.py:600
  23.0 2.8 %gain_stage.2.refs_0_ = f32[256,128]{1,0:T(8,128)S(1)} custom-call(s32[1]{0:T(128)} %bitcast.8.where_ref, f32[16,5,8,128]{3,2,1,0:T(8,128)S(1)} %all-to-all-done.packet_ref), custom_call_target="tpu_custom_call" | custom-call | tf_op jit(solution)/shard_map/gain_stage/pallas_call | solution.py:390
  25.8 0.2 collective-permute-start
  26.0 1.0 %gain_stage.3 = (f32[64,128]{1,0:T(8,128)S(1)}, f32[320,128]{1,0:T(8,128)S(1)}) custom-call(s32[1]{0:T(128)} %bitcast.8.where_ref, f32[16,5,8,128]{3,2,1,0:T(8,128)S(1)} %all-to-all-done.packet_ref, f32[256,128]{1,0:T(8,128)S(1)} %gain_stage.2.refs_0_), custom_call_target="tpu_custom_call" | custom-call | tf_op jit(solution)/shard_map/gain_stage/pallas_call | solution.py:390
  27.1 1.9 %collective-permute-start.1 = (f32[64,128]{1,0:T(8,128)S(1)}, f32[64,128]{1,0:T(8,128)S(1)}, u32[]{:S(2)}, u32[]{:S(2)}) collective-permute-start(f32[64,128]{1,0:T(8,128)S(1)} %get-tuple-element.18), channel_id=1, source_target_pairs={{0,4},{1,3},{2,6},{3,1},{4,0},{5,7},{6,2},{7,5},{8,12},{9,11},{10,... | collective-permute-start | bytes 98312 | tf_op jit(solution)/shard_map/ppermute | solution.py:623
  29.0 0.0 collective-permute-start.2
  29.0 0.8 %vote_stage.3.refs_0_ = f32[768,128]{1,0:T(8,128)S(1)} custom-call(f32[16,5,8,128]{3,2,1,0:T(8,128)S(1)} %all-to-all-done.packet_ref), custom_call_target="tpu_custom_call" | custom-call | flops 20000000 | bytes 400000 | tf_op jit(solution)/shard_map/vote_stage/pallas_call | solution.py:460
  29.8 1.0 %collective-permute-done.refs_1_ = f32[256,128]{1,0:T(8,128)S(1)} collective-permute-done((f32[256,128]{1,0:T(8,128)S(1)}, f32[256,128]{1,0:T(8,128)S(1)}, u32[]{:S(2)}, u32[]{:S(2)}) %collective-permute-start) | collective-permute-done | bytes 131104 | tf_op jit(solution)/shard_map/ppermute | solution.py:623
  30.8 0.8 %vote_stage.4.refs_0_ = f32[768,128]{1,0:T(8,128)S(1)} custom-call(f32[16,5,8,128]{3,2,1,0:T(8,128)S(1)} %all-to-all-done.packet_ref, f32[768,128]{1,0:T(8,128)S(1)} %vote_stage.3.refs_0_), custom_call_target="tpu_custom_call" | custom-call | flops 20000000 | bytes 400000 | tf_op jit(solution)/shard_map/vote_stage/pallas_call | solution.py:460
  31.6 1.4 %vote_stage.5 = s32[32,700]{1,0:T(8,128)} custom-call(f32[16,5,8,128]{3,2,1,0:T(8,128)S(1)} %all-to-all-done.packet_ref, f32[768,128]{1,0:T(8,128)S(1)} %vote_stage.4.refs_0_), custom_call_target="tpu_custom_call" | custom-call | flops 20000000 | bytes 400000 | tf_op jit(solution)/shard_map/vote_stage/pallas_call | solution.py:460
  33.0 0.0 collective-permute-done.1.refs_2_
  33.0 0.1 collective-permute-start.5
  33.1 1.1 %collective-permute-start.3 = (f32[256,128]{1,0:T(8,128)S(1)}, f32[256,128]{1,0:T(8,128)S(1)}, u32[]{:S(2)}, u32[]{:S(2)}) collective-permute-start(f32[256,128]{1,0:T(8,128)S(1)} %collective-permute-done.refs_1_), channel_id=1, source_target_pairs={{0,2},{1,5},{2,0},{3,7},{4,6},{5,1},{6,4},{7,3},{8,10},{9,13},{10,... | collective-permute-start | bytes 393224 | tf_op jit(solution)/shard_map/ppermute | solution.py:623
  34.1 0.2 collective-permute-done.2.refs_3_
  34.3 0.0 collective-permute-start.6
  34.3 3.8 %collective-permute-done.3.refs_4_ = f32[256,128]{1,0:T(8,128)S(1)} collective-permute-done((f32[256,128]{1,0:T(8,128)S(1)}, f32[256,128]{1,0:T(8,128)S(1)}, u32[]{:S(2)}, u32[]{:S(2)}) %collective-permute-start.3) | collective-permute-done | bytes 131104 | tf_op jit(solution)/shard_map/ppermute | solution.py:623
  38.1 0.0 collective-permute-start.7
  38.1 1.0 %collective-permute-start.4 = (f32[64,128]{1,0:T(8,128)S(1)}, f32[64,128]{1,0:T(8,128)S(1)}, u32[]{:S(2)}, u32[]{:S(2)}) collective-permute-start(f32[64,128]{1,0:T(8,128)S(1)} %collective-permute-done.1.refs_2_), channel_id=1, source_target_pairs={{0,2},{1,5},{2,0},{3,7},{4,6},{5,1},{6,4},{7,3},{8,10},{9,13},{10,... | collective-permute-start | bytes 98312 | tf_op jit(solution)/shard_map/ppermute | solution.py:623
  39.1 2.9 %collective-permute-done.4.refs_5_ = f32[64,128]{1,0:T(8,128)S(1)} collective-permute-done((f32[64,128]{1,0:T(8,128)S(1)}, f32[64,128]{1,0:T(8,128)S(1)}, u32[]{:S(2)}, u32[]{:S(2)}) %collective-permute-start.4) | collective-permute-done | bytes 32800 | tf_op jit(solution)/shard_map/ppermute | solution.py:623
  42.0 0.0 collective-permute-start.8
  42.0 1.2 %collective-permute-done.8.refs_9_ = f32[64,128]{1,0:T(8,128)S(1)} collective-permute-done((f32[64,128]{1,0:T(8,128)S(1)}, f32[64,128]{1,0:T(8,128)S(1)}, u32[]{:S(2)}, u32[]{:S(2)}) %collective-permute-start.8) | collective-permute-done | bytes 32800 | tf_op jit(solution)/shard_map/ppermute | solution.py:630
  43.2 0.0 collective-permute-done.6.refs_7_
  43.2 0.0 collective-permute-done.7.refs_8_
  43.2 0.0 collective-permute-done.5.refs_6_
  43.2 1.2 %place_stage.1 = f32[1280,256]{1,0:T(8,128)} custom-call(s32[1]{0:T(128)} %bitcast.8.where_ref, f32[320,128]{1,0:T(8,128)S(1)} %get-tuple-element.16.refs_0_, f32[256,128]{1,0:T(8,128)S(1)} %collective-permute-done.refs_1_, f32[64,128]{1,0:T(8,128)S(1)} %collective-permute-done.1.refs_2_, f32[320,128]{1,0:T(8,128)S(1)} %collective-permute-done.2.refs_3_, ...), custom_call_target="tpu_custom_call" | custom-call | tf_op jit(solution)/shard_map/place_stage/pallas_call | solution.py:543
  (1 shorter events, 0.0 us)
Async XLA Ops:
  4.5 18.5 %all-to-all-start = ((f32[16,5,8,128]{3,2,1,0:T(8,128)}), f32[16,5,8,128]{3,2,1,0:T(8,128)S(1)}, u32[]{:S(2)}, u32[]{:S(2)}) async-start(f32[16,5,8,128]{3,2,1,0:T(8,128)} %get-tuple-element.15), calls=%async_computation | async-start | bytes 655360 | tf_op jit(solution)/shard_map/all_to_all | solution.py:600
  25.8 5.0 %collective-permute-start = (f32[256,128]{1,0:T(8,128)S(1)}, f32[256,128]{1,0:T(8,128)S(1)}, u32[]{:S(2)}, u32[]{:S(2)}) collective-permute-start(f32[256,128]{1,0:T(8,128)S(1)} %gain_stage.2.refs_0_), channel_id=1, source_target_pairs={{0,4},{1,3},{2,6},{3,1},{4,0},{5,7},{6,2},{7,5},{8,12},{9,11},{10,... | collective-permute-start | bytes 393224 | tf_op jit(solution)/shard_map/ppermute | solution.py:623
  27.1 5.9 %collective-permute-start.1 = (f32[64,128]{1,0:T(8,128)S(1)}, f32[64,128]{1,0:T(8,128)S(1)}, u32[]{:S(2)}, u32[]{:S(2)}) collective-permute-start(f32[64,128]{1,0:T(8,128)S(1)} %get-tuple-element.18), channel_id=1, source_target_pairs={{0,4},{1,3},{2,6},{3,1},{4,0},{5,7},{6,2},{7,5},{8,12},{9,11},{10,... | collective-permute-start | bytes 98312 | tf_op jit(solution)/shard_map/ppermute | solution.py:623
  29.0 5.3 %collective-permute-start.2 = (f32[320,128]{1,0:T(8,128)S(1)}, f32[320,128]{1,0:T(8,128)S(1)}, u32[]{:S(2)}, u32[]{:S(2)}) collective-permute-start(f32[320,128]{1,0:T(8,128)S(1)} %get-tuple-element.16.refs_0_), channel_id=1, source_target_pairs={{0,2},{1,5},{2,0},{3,7},{4,6},{5,1},{6,4},{7,3},{8,10},{9,13},{10,... | collective-permute-start | bytes 491528 | tf_op jit(solution)/shard_map/ppermute | solution.py:623
  33.0 10.2 %collective-permute-start.5 = (f32[640,128]{1,0:T(8,128)S(1)}, f32[640,128]{1,0:T(8,128)S(1)}, u32[]{:S(2)}, u32[]{:S(2)}) collective-permute-start(f32[640,128]{1,0:T(8,128)S(1)} %pack_stage.1), channel_id=1, source_target_pairs={{0,1},{1,0},{2,3},{3,2},{4,5},{5,4},{6,7},{7,6},{8,9},{9,8},{10,11... | collective-permute-start | bytes 983048 | tf_op jit(solution)/shard_map/ppermute | solution.py:630
  33.1 5.0 %collective-permute-start.3 = (f32[256,128]{1,0:T(8,128)S(1)}, f32[256,128]{1,0:T(8,128)S(1)}, u32[]{:S(2)}, u32[]{:S(2)}) collective-permute-start(f32[256,128]{1,0:T(8,128)S(1)} %collective-permute-done.refs_1_), channel_id=1, source_target_pairs={{0,2},{1,5},{2,0},{3,7},{4,6},{5,1},{6,4},{7,3},{8,10},{9,13},{10,... | collective-permute-start | bytes 393224 | tf_op jit(solution)/shard_map/ppermute | solution.py:623
  34.3 8.9 %collective-permute-start.6 = (f32[320,128]{1,0:T(8,128)S(1)}, f32[320,128]{1,0:T(8,128)S(1)}, u32[]{:S(2)}, u32[]{:S(2)}) collective-permute-start(f32[320,128]{1,0:T(8,128)S(1)} %collective-permute-done.2.refs_3_), channel_id=1, source_target_pairs={{0,1},{1,0},{2,3},{3,2},{4,5},{5,4},{6,7},{7,6},{8,9},{9,8},{10,11... | collective-permute-start | bytes 491528 | tf_op jit(solution)/shard_map/ppermute | solution.py:630
  38.1 5.1 %collective-permute-start.7 = (f32[256,128]{1,0:T(8,128)S(1)}, f32[256,128]{1,0:T(8,128)S(1)}, u32[]{:S(2)}, u32[]{:S(2)}) collective-permute-start(f32[256,128]{1,0:T(8,128)S(1)} %collective-permute-done.3.refs_4_), channel_id=1, source_target_pairs={{0,1},{1,0},{2,3},{3,2},{4,5},{5,4},{6,7},{7,6},{8,9},{9,8},{10,11... | collective-permute-start | bytes 393224 | tf_op jit(solution)/shard_map/ppermute | solution.py:630
  38.1 3.9 %collective-permute-start.4 = (f32[64,128]{1,0:T(8,128)S(1)}, f32[64,128]{1,0:T(8,128)S(1)}, u32[]{:S(2)}, u32[]{:S(2)}) collective-permute-start(f32[64,128]{1,0:T(8,128)S(1)} %collective-permute-done.1.refs_2_), channel_id=1, source_target_pairs={{0,2},{1,5},{2,0},{3,7},{4,6},{5,1},{6,4},{7,3},{8,10},{9,13},{10,... | collective-permute-start | bytes 98312 | tf_op jit(solution)/shard_map/ppermute | solution.py:623
  42.0 1.2 %collective-permute-start.8 = (f32[64,128]{1,0:T(8,128)S(1)}, f32[64,128]{1,0:T(8,128)S(1)}, u32[]{:S(2)}, u32[]{:S(2)}) collective-permute-start(f32[64,128]{1,0:T(8,128)S(1)} %collective-permute-done.4.refs_5_), channel_id=1, source_target_pairs={{0,1},{1,0},{2,3},{3,2},{4,5},{5,4},{6,7},{7,6},{8,9},{9,8},{10,11... | collective-permute-start | bytes 98312 | tf_op jit(solution)/shard_map/ppermute | solution.py:630
